TPU v7x, 32 devices: a whole 2x2x4 slice. The times are simulated.
32 devices in a mesh: dp: 4 (over z), row: 2 (over x), col: 4 (over y, core).
Axes of the slice: x: 2, y: 2, z: 4, core: 2. Of those that a mesh axis runs over, the one named last changes fastest.
Arguments:
- images: bfloat16 [32, 729, 1152], P(('dp', 'row', 'col')), may hold values from -6 to 6
- cotangent: bfloat16 [32, 729, 1152], P(('dp', 'row', 'col')), may hold values from -6 to 6
- first_gain: float32 [1152], replicated, may hold values from 0.25 to 1.75
- first_shift: float32 [1152], replicated, may hold values from -3 to 3
- query_weight: bfloat16 [1152, 1152], P('row', 'col'), may hold values from -0.1875 to 0.1875
- query_bias: float32 [1152], P('col'), may hold values from -3 to 3
- key_weight: bfloat16 [1152, 1152], P('row', 'col'), may hold values from -0.1875 to 0.1875
- value_weight: bfloat16 [1152, 1152], P('row', 'col'), may hold values from -0.1875 to 0.1875
- value_bias: float32 [1152], P('col'), may hold values from -3 to 3
- output_weight: bfloat16 [1152, 1152], P('col', 'row'), may hold values from -0.75 to 0.75
- output_bias: float32 [1152], replicated, may hold values from -3 to 3
- second_gain: float32 [1152], replicated, may hold values from 0.1 to 1.9
- second_shift: float32 [1152], replicated, may hold values from -3 to 3
- expand_weight: bfloat16 [1152, 4304], P('row', 'col'), may hold values from -0.1875 to 0.1875
- expand_bias: float32 [4304], P('col'), may hold values from -3 to 3
- shrink_weight: bfloat16 [4304, 1152], P('col', 'row'), may hold values from -0.1875 to 0.1875
- shrink_bias: float32 [1152], replicated, may hold values from -3 to 3
Outputs:
- layer_out: bfloat16 [32, 729, 1152], P(('dp', 'row', 'col'))
- grad_images: bfloat16 [32, 729, 1152], P(('dp', 'row', 'col'))
- grad_first_gain: float32 [1152], replicated
- grad_first_shift: float32 [1152], replicated
- grad_query_weight: float32 [1152, 1152], P('row', 'col')
- grad_query_bias: float32 [1152], P('col')
- grad_key_weight: float32 [1152, 1152], P('row', 'col')
- grad_value_weight: float32 [1152, 1152], P('row', 'col')
- grad_value_bias: float32 [1152], P('col')
- grad_output_weight: float32 [1152, 1152], P('col', 'row')
- grad_output_bias: float32 [1152], replicated
- grad_second_gain: float32 [1152], replicated
- grad_second_shift: float32 [1152], replicated
- grad_expand_weight: float32 [1152, 4304], P('row', 'col')
- grad_expand_bias: float32 [4304], P('col')
- grad_shrink_weight: float32 [4304, 1152], P('col', 'row')
- grad_shrink_bias: float32 [1152], replicated
All inputs are finite; a program needn't handle non-finite values.
Results may differ from a plain program's by a relative error of at most 0.038.
Values may be sent and summed in bfloat16 or wider, within the bound.
A program may use at most 448 MiB of HBM per device.

v0:
```python
import jax
import jax.numpy as jnp
from jax import lax
from jax.sharding import PartitionSpec as P

HEAD_DIM = 72
EPS = 1e-06
contract_last = (((2,), (1,)), ((), ()))
contract_rows = (((0, 1), (0, 1)), ((), ()))


def gelu_tanh(value):
    return jax.nn.gelu(value, approximate=True)


def norm_forward(stream, gain, shift):
    average = jnp.mean(stream, axis=-1, keepdims=True)
    second = jnp.mean(stream * stream, axis=-1, keepdims=True)
    inverse = lax.rsqrt(second - average * average + EPS)
    normed = (stream - average) * inverse
    return (normed, inverse, (normed * gain + shift).astype(jnp.bfloat16))


def norm_backward(grad_out, normed, inverse, gain):
    scaled = grad_out * gain
    first = jnp.mean(scaled, axis=-1, keepdims=True)
    second = jnp.mean(scaled * normed, axis=-1, keepdims=True)
    return inverse * (scaled - first - normed * second)


def spread(block):
    feature_part = lax.all_to_all(block, "row", split_axis=2, concat_axis=0, tiled=True)
    return lax.all_gather(feature_part, "col", axis=0, tiled=True)


def join_back(summed):
    return lax.all_to_all(
        summed.astype(jnp.bfloat16), "row", split_axis=0, concat_axis=2, tiled=True
    ).astype(summed.dtype)


def project_in(normed_bf, weight):
    gathered = spread(normed_bf)
    summed = lax.psum_scatter(
        jnp.dot(gathered, weight, preferred_element_type=jnp.float32).astype(jnp.bfloat16),
        "row",
        scatter_dimension=0,
        tiled=True,
    ).astype(jnp.float32)
    return (summed, gathered)


def project_out(block_bf, weight):
    partial_sums = jnp.dot(
        lax.all_gather(block_bf, "row", axis=0, tiled=True),
        weight,
        preferred_element_type=jnp.float32,
    )
    return join_back(
        lax.psum_scatter(
            partial_sums.astype(jnp.bfloat16), "col", scatter_dimension=0, tiled=True
        ).astype(jnp.float32)
    )


def back_out(grad_bf, acts_bf, weight):
    grads_all = spread(grad_bf)
    grad_acts = lax.psum_scatter(
        lax.dot_general(
            grads_all, weight, contract_last, preferred_element_type=jnp.float32
        ).astype(jnp.bfloat16),
        "row",
        scatter_dimension=0,
        tiled=True,
    ).astype(jnp.float32)
    grad_weight = lax.dot_general(
        lax.all_gather(acts_bf, "row", axis=0, tiled=True),
        grads_all,
        contract_rows,
        preferred_element_type=jnp.float32,
    )
    return (grad_acts, grad_weight)


def back_in(grad_bf, weight, normed_bf):
    inputs_all = spread(normed_bf)
    piece = lax.all_gather(grad_bf, "row", axis=0, tiled=True)
    contrib = lax.dot_general(piece, weight, contract_last, preferred_element_type=jnp.float32)
    partial_sums = contrib
    weight_grad = lax.dot_general(
        inputs_all, piece, contract_rows, preferred_element_type=jnp.float32
    )
    partial_sums, weight_grad = (partial_sums, weight_grad)
    grad_inputs = join_back(
        lax.psum_scatter(
            partial_sums.astype(jnp.bfloat16), "col", scatter_dimension=0, tiled=True
        ).astype(jnp.float32)
    )
    return (grad_inputs, weight_grad)


def split_heads(block):
    return block.reshape(block.shape[0], block.shape[1] // HEAD_DIM, HEAD_DIM)


def head_scores(queries, key_rows):
    scores = jnp.einsum(
        "qhd,khd->hqk",
        split_heads(queries),
        split_heads(key_rows),
        preferred_element_type=jnp.float32,
    )
    return scores * HEAD_DIM ** (-0.5)


def attend(queries, key_rows, value_rows):

    def one_image(triple):
        scores = head_scores(triple[0], triple[1])
        peak = jnp.max(scores, axis=-1, keepdims=True)
        log_total = peak + jnp.log(jnp.sum(jnp.exp(scores - peak), axis=-1, keepdims=True))
        attention = jnp.exp(scores - log_total).astype(jnp.bfloat16)
        mixed = jnp.einsum(
            "hqk,khd->qhd", attention, split_heads(triple[2]), preferred_element_type=jnp.float32
        )
        return (mixed.reshape(triple[0].shape).astype(jnp.bfloat16), log_total)

    return lax.map(one_image, (queries, key_rows, value_rows))


def attend_back(queries, key_rows, value_rows, attended, log_total, grad_attended):
    scale = HEAD_DIM ** (-0.5)

    def one_image(group):
        image_q, image_k, image_v, image_out, image_total, image_grad = group
        attention = jnp.exp(head_scores(image_q, image_k) - image_total)
        grad_heads = split_heads(image_grad)
        grad_probs = jnp.einsum(
            "qhd,khd->hqk", grad_heads, split_heads(image_v), preferred_element_type=jnp.float32
        )
        delta = jnp.einsum(
            "qhd,qhd->hq", grad_heads, split_heads(image_out), preferred_element_type=jnp.float32
        )[..., None]
        grad_scores = (attention * (grad_probs - delta)).astype(jnp.bfloat16)
        grad_queries = (
            jnp.einsum(
                "hqk,khd->qhd",
                grad_scores,
                split_heads(image_k),
                preferred_element_type=jnp.float32,
            )
            * scale
        )
        grad_keys = (
            jnp.einsum(
                "hqk,qhd->khd",
                grad_scores,
                split_heads(image_q),
                preferred_element_type=jnp.float32,
            )
            * scale
        )
        grad_values = jnp.einsum(
            "hqk,qhd->khd",
            attention.astype(jnp.bfloat16),
            grad_heads,
            preferred_element_type=jnp.float32,
        )
        shape = image_q.shape
        return (grad_queries.reshape(shape), grad_keys.reshape(shape), grad_values.reshape(shape))

    return lax.map(one_image, (queries, key_rows, value_rows, attended, log_total, grad_attended))


def feature_terms(grad_input1, normed1, grad_middle, grad_input2, normed2, grad_result):
    token_axes = (0, 1)
    return (
        jnp.sum(grad_input1 * normed1, axis=token_axes),
        jnp.sum(grad_input1, axis=token_axes),
        jnp.sum(grad_middle, axis=token_axes),
        jnp.sum(grad_input2 * normed2, axis=token_axes),
        jnp.sum(grad_input2, axis=token_axes),
        jnp.sum(grad_result, axis=token_axes),
    )


def embed_part(part_sum):
    start = lax.axis_index("col") * part_sum.shape[0]
    whole = jnp.zeros((part_sum.shape[0] * lax.axis_size("col"),), jnp.float32)
    return lax.dynamic_update_slice_in_dim(whole, part_sum, start, 0)


def grid_layer(images, cotangent, params):
    (
        first_gain,
        first_shift,
        query_weight,
        query_bias,
        key_weight,
        value_weight,
        value_bias,
        output_weight,
        output_bias,
        second_gain,
        second_shift,
        expand_weight,
        expand_bias,
        shrink_weight,
        shrink_bias,
    ) = params
    width = query_weight.shape[1]
    joined = jnp.concatenate((query_weight, key_weight, value_weight), axis=1)
    stream = images.astype(jnp.float32)
    normed1, inverse1, input1 = norm_forward(stream, first_gain, first_shift)
    projected, kept_first = project_in(input1, joined)
    queries = (projected[..., :width] + query_bias).astype(jnp.bfloat16)
    key_rows = projected[..., width : 2 * width].astype(jnp.bfloat16)
    value_rows = (projected[..., 2 * width :] + value_bias).astype(jnp.bfloat16)
    attended, log_total = attend(queries, key_rows, value_rows)
    middle = stream + project_out(attended, output_weight) + output_bias
    normed2, inverse2, input2 = norm_forward(middle, second_gain, second_shift)
    expanded, kept_second = project_in(input2, expand_weight)
    before = expanded + expand_bias
    hidden = gelu_tanh(before).astype(jnp.bfloat16)
    result = middle + project_out(hidden, shrink_weight) + shrink_bias
    grad_result = cotangent.astype(jnp.float32)
    grad_hidden, grad_shrink = back_out(cotangent, hidden, shrink_weight)
    gelu_back = jax.vjp(gelu_tanh, before)[1]
    grad_before = gelu_back(grad_hidden)[0]
    grad_input2, grad_expand = back_in(grad_before.astype(jnp.bfloat16), expand_weight, input2)
    grad_middle = grad_result + norm_backward(grad_input2, normed2, inverse2, second_gain)
    grad_attended, grad_output = back_out(grad_middle.astype(jnp.bfloat16), attended, output_weight)
    grad_queries, grad_keys, grad_values = attend_back(
        queries, key_rows, value_rows, attended, log_total, grad_attended.astype(jnp.bfloat16)
    )
    grad_joined_rows = jnp.concatenate((grad_queries, grad_keys, grad_values), axis=-1).astype(
        jnp.bfloat16
    )
    grad_input1, grad_joined = back_in(grad_joined_rows, joined, input1)
    grad_stream = grad_middle + norm_backward(grad_input1, normed1, inverse1, first_gain)
    token_axes = (0, 1)
    features = feature_terms(grad_input1, normed1, grad_middle, grad_input2, normed2, grad_result)
    biases = (
        embed_part(jnp.sum(grad_queries, axis=token_axes)),
        embed_part(jnp.sum(grad_values, axis=token_axes)),
        embed_part(jnp.sum(grad_before, axis=token_axes)),
    )
    blocks = (
        grad_joined[:, :width],
        grad_joined[:, width : 2 * width],
        grad_joined[:, 2 * width :],
        grad_output,
        grad_expand,
        grad_shrink,
    )
    return (result, grad_stream, features, biases, blocks)


def shards(
    images,
    cotangent,
    first_gain,
    first_shift,
    query_weight,
    query_bias,
    key_weight,
    value_weight,
    value_bias,
    output_weight,
    output_bias,
    second_gain,
    second_shift,
    expand_weight,
    expand_bias,
    shrink_weight,
    shrink_bias,
):
    params = (
        first_gain,
        first_shift,
        query_weight,
        query_bias,
        key_weight,
        value_weight,
        value_bias,
        output_weight,
        output_bias,
        second_gain,
        second_shift,
        expand_weight,
        expand_bias,
        shrink_weight,
        shrink_bias,
    )
    result, grad_stream, features, biases, blocks = grid_layer(images, cotangent, params)
    totals = lax.psum(
        (
            features[0],
            features[1],
            features[2],
            features[3],
            features[4],
            features[5],
            biases[0],
            biases[1],
            biases[2],
        ),
        ("dp", "row", "col"),
    )
    col_index = lax.axis_index("col")
    query_part = query_bias.shape[0]
    expand_part = expand_bias.shape[0]
    query_bias_grad = lax.dynamic_slice_in_dim(totals[6], col_index * query_part, query_part, 0)
    value_bias_grad = lax.dynamic_slice_in_dim(totals[7], col_index * query_part, query_part, 0)
    expand_bias_grad = lax.dynamic_slice_in_dim(totals[8], col_index * expand_part, expand_part, 0)
    weight_totals = (
        lax.psum(blocks[0].astype(jnp.bfloat16), "dp").astype(jnp.float32),
        lax.psum(blocks[1].astype(jnp.bfloat16), "dp").astype(jnp.float32),
        lax.psum(blocks[2].astype(jnp.bfloat16), "dp").astype(jnp.float32),
        lax.psum(blocks[3].astype(jnp.bfloat16), "dp").astype(jnp.float32),
        lax.psum(blocks[4].astype(jnp.bfloat16), "dp").astype(jnp.float32),
        lax.psum(blocks[5].astype(jnp.bfloat16), "dp").astype(jnp.float32),
    )
    return (
        result.astype(jnp.bfloat16),
        grad_stream.astype(jnp.bfloat16),
        totals[0],
        totals[1],
        weight_totals[0],
        query_bias_grad,
        weight_totals[1],
        weight_totals[2],
        value_bias_grad,
        weight_totals[3],
        totals[2],
        totals[3],
        totals[4],
        weight_totals[4],
        expand_bias_grad,
        weight_totals[5],
        totals[5],
    )


def solution(mesh):
    placed = (
        P(("dp", "row", "col"), None, None),
        P(("dp", "row", "col"), None, None),
        P(),
        P(),
        P("row", "col"),
        P("col"),
        P("row", "col"),
        P("row", "col"),
        P("col"),
        P("col", "row"),
        P(),
        P(),
        P(),
        P("row", "col"),
        P("col"),
        P("col", "row"),
        P(),
    )
    return jax.shard_map(
        shards,
        mesh=mesh,
        in_specs=placed,
        out_specs=(
            P(("dp", "row", "col"), None, None),
            P(("dp", "row", "col"), None, None),
            P(),
            P(),
            P("row", "col"),
            P("col"),
            P("row", "col"),
            P("row", "col"),
            P("col"),
            P("col", "row"),
            P(),
            P(),
            P(),
            P("row", "col"),
            P("col"),
            P("col", "row"),
            P(),
        ),
        check_vma=False,
    )
```

profile of v0, /device:TPU:0, one launch (start us, length us, event | category | flops | bytes accessed | tf_op | source)
XLA Modules:
  0.0 2109.9 jit_solution(17329852611036355849)
XLA Ops:
  37.9 25.5 %all_to_all.118 = bf16[2,2,209952]{2,1,0:T(2,128)(2,1)S(1)} all-to-all(bf16[2,2,209952]{2,1,0:T(2,128)(2,1)} %reshape.487), channel_id=1, replica_groups=mesh['dp'=4,'row'=2,'col'=4] {'row'}, dimensions={0} | all-to-all | bytes 3359232 | tf_op jit(solution)/shard_map/all_to_all | solution.py:32
  74.0 50.2 %all-gather.21.cloned.1.call-done = bf16[8,1,729,576]{2,3,1,0:T(8,128)(2,1)} async-done(((bf16[2,1,729,576]{2,3,1,0:T(8,128)(2,1)}), bf16[8,1,729,576]{2,3,1,0:T(8,128)(2,1)}) %all-gather.21.cloned.1.call-update) | async-done | bytes 6718480 | tf_op jit(solution)/shard_map/all_gather | solution.py:33
  124.3 14.3 fusion.37
  138.8 122.5 %reduce-scatter.9.cloned.1.call-done = bf16[4,729,864]{2,1,0:T(8,128)(2,1)} async-done(((bf16[8,729,864]{2,1,0:T(8,128)(2,1)}), bf16[4,729,864]{2,1,0:T(8,128)(2,1)}) %reduce-scatter.9.cloned.1.call-update) | async-done | bytes 5038864 | tf_op jit(solution)/shard_map/reduce_scatter | solution.py:44
  283.5 32.8 %while.26 = (s32[]{:T(128)}, bf16[4,729,288]{1,2,0:T(8,128)(2,1)}, f32[4,4,729,1]{2,1,3,0:T(4,128)}, bf16[4,729,288]{1,2,0:T(8,128)(2,1)}, bf16[4,729,288]{1,2,0...) while((s32[]{:T(128)}, bf16[4,729,288]{1,2,0:T(8,128)(2,1)}, f32[4,4,729,1]{2,1,3,0:T(4,128)}, ...), condition=%wide.region_6.7_spmd, body=%wide.region_3.6_spmd.sunk | while | flops 629433152 | bytes 30664516 | solution.py:128
  316.6 49.3 %all-gather.13.cloned.1.call-done = bf16[8,729,288]{1,2,0:T(8,128)(2,1)} async-done(((bf16[4,729,288]{1,2,0:T(8,128)(2,1)}), bf16[8,729,288]{1,2,0:T(8,128)(2,1)}) %all-gather.13.cloned.1.call-update) | async-done | bytes 3359248 | tf_op jit(solution)/shard_map/all_gather | solution.py:55
  401.5 24.2 %all_to_all.119 = bf16[2,2,209952]{2,1,0:T(2,128)(2,1)S(1)} all-to-all(bf16[2,2,209952]{2,1,0:T(2,128)(2,1)} %reshape.489), channel_id=1, replica_groups=mesh['dp'=4,'row'=2,'col'=4] {'row'}, dimensions={0} | all-to-all | bytes 3359232 | tf_op jit(solution)/shard_map/all_to_all | solution.py:32
  439.0 25.5 %all_to_all.120 = bf16[2,729,576]{1,2,0:T(8,128)(2,1)S(1)} all-to-all(bf16[2,729,576]{1,2,0:T(8,128)(2,1)} %reduce-scatter.11.cloned.1.call-done), channel_id=1, replica_groups=mesh['dp'=4,'row'=2,'col'=4] {'row'}, dimensions={0} | all-to-all | bytes 3359232 | tf_op jit(solution)/shard_map/all_to_all | solution.py:37
  502.3 23.4 %all_to_all.121 = bf16[2,2,209952]{2,1,0:T(2,128)(2,1)S(1)} all-to-all(bf16[2,2,209952]{2,1,0:T(2,128)(2,1)} %reshape.491), channel_id=1, replica_groups=mesh['dp'=4,'row'=2,'col'=4] {'row'}, dimensions={0} | all-to-all | bytes 3359232 | tf_op jit(solution)/shard_map/all_to_all | solution.py:32
  535.3 16.6 convolution_convert_fusion
  551.9 33.1 %all-gather.23.cloned.1.call-done = bf16[8,1,729,576]{2,3,1,0:T(8,128)(2,1)} async-done(((bf16[2,1,729,576]{2,3,1,0:T(8,128)(2,1)}), bf16[8,1,729,576]{2,3,1,0:T(8,128)(2,1)}) %all-gather.23.cloned.1.call-update) | async-done | bytes 6718480 | tf_op jit(solution)/shard_map/all_gather | solution.py:33
  585.1 16.6 convolution_convert_fusion.1
  601.7 137.7 %reduce-scatter.17.cloned.1.call-done = bf16[4,729,1076]{1,2,0:T(8,128)(2,1)} async-done(((bf16[8,729,1076]{1,2,0:T(8,128)(2,1)}), bf16[4,729,1076]{1,2,0:T(8,128)(2,1)}) %reduce-scatter.17.cloned.1.call-update) | async-done | bytes 6275248 | tf_op jit(solution)/shard_map/reduce_scatter | solution.py:68
  739.4 154.3 %reduce-scatter.13.cloned.1.call-done = bf16[4,729,1076]{1,2,0:T(8,128)(2,1)} async-done(((bf16[8,729,1076]{1,2,0:T(8,128)(2,1)}), bf16[4,729,1076]{1,2,0:T(8,128)(2,1)}) %reduce-scatter.13.cloned.1.call-update) | async-done | bytes 6275248 | tf_op jit(solution)/shard_map/reduce_scatter | solution.py:44
  893.7 17.1 fusion.91
  911.7 159.4 %all-gather.17.cloned.1.call-done = bf16[8,729,1076]{1,2,0:T(8,128)(2,1)} async-done(((bf16[4,729,1076]{1,2,0:T(8,128)(2,1)}), bf16[8,729,1076]{1,2,0:T(8,128)(2,1)}) %all-gather.17.cloned.1.call-update) | async-done | bytes 12550480 | tf_op jit(solution)/shard_map/all_gather | solution.py:87
  1071.0 15.9 convolution_convert_fusion.2
  1087.0 145.5 %all-gather.15.cloned.1.call-done = bf16[8,729,1076]{1,2,0:T(8,128)(2,1)} async-done(((bf16[4,729,1076]{1,2,0:T(8,128)(2,1)}), bf16[8,729,1076]{1,2,0:T(8,128)(2,1)}) %all-gather.15.cloned.1.call-update) | async-done | bytes 12550480 | tf_op jit(solution)/shard_map/all_gather | solution.py:55
  1232.5 15.9 convolution_convert_fusion.3
  1248.4 50.8 %reduce-scatter.19.cloned.1.call-done = bf16[2,729,576]{1,2,0:T(8,128)(2,1)} async-done(((bf16[8,729,576]{1,2,0:T(8,128)(2,1)}), bf16[2,729,576]{1,2,0:T(8,128)(2,1)}) %reduce-scatter.19.cloned.1.call-update) | async-done | bytes 1679632 | tf_op jit(solution)/shard_map/reduce_scatter | solution.py:95
  1303.1 62.8 %reduce-scatter.15.cloned.1.call-done = bf16[2,729,576]{1,2,0:T(8,128)(2,1)} async-done(((bf16[8,729,576]{1,2,0:T(8,128)(2,1)}), bf16[2,729,576]{1,2,0:T(8,128)(2,1)}) %reduce-scatter.15.cloned.1.call-update) | async-done | bytes 1679632 | tf_op jit(solution)/shard_map/reduce_scatter | solution.py:60
  1437.7 23.0 %all_to_all.122 = bf16[2,2,209952]{2,1,0:T(2,128)(2,1)} all-to-all(bf16[2,2,209952]{2,1,0:T(2,128)(2,1)S(1)} %reshape.493), channel_id=1, replica_groups=mesh['dp'=4,'row'=2,'col'=4] {'row'}, dimensions={0} | all-to-all | bytes 3359232 | tf_op jit(solution)/shard_map/all_to_all | solution.py:32
  1468.0 49.9 %all-gather.27.cloned.1.call-done = bf16[8,1,729,576]{2,3,1,0:T(8,128)(2,1)} async-done(((bf16[2,1,729,576]{2,3,1,0:T(8,128)(2,1)}), bf16[8,1,729,576]{2,3,1,0:T(8,128)(2,1)}) %all-gather.27.cloned.1.call-update) | async-done | bytes 6718480 | tf_op jit(solution)/shard_map/all_gather | solution.py:33
  1525.7 47.8 %reduce-scatter.21.cloned.1.call-done = bf16[4,729,288]{1,2,0:T(8,128)(2,1)} async-done(((bf16[8,729,288]{1,2,0:T(8,128)(2,1)}), bf16[4,729,288]{1,2,0:T(8,128)(2,1)}) %reduce-scatter.21.cloned.1.call-update) | async-done | bytes 1679632 | tf_op jit(solution)/shard_map/reduce_scatter | solution.py:68
  1573.5 70.2 %while.27 = (s32[]{:T(128)}, f32[4,729,288]{1,2,0:T(8,128)}, bf16[4,729,288]{1,2,0:T(8,128)(2,1)}, f32[4,729,288]{1,2,0:T(8,128)S(1)}, bf16[4,729,288]{1,2,0:T(8...) while((s32[]{:T(128)}, f32[4,729,288]{1,2,0:T(8,128)}, ...), condition=%wide.region_18.19_spmd, body=%wide.region_17.18_spmd.sunk | while | flops 1549022848 | bytes 52812796 | solution.py:172
  1659.2 130.3 %all-gather.19.cloned.1.call-done = bf16[8,729,864]{2,1,0:T(8,128)(2,1)} async-done(((bf16[4,729,864]{2,1,0:T(8,128)(2,1)}), bf16[8,729,864]{2,1,0:T(8,128)(2,1)}) %all-gather.19.cloned.1.call-update) | async-done | bytes 10077712 | tf_op jit(solution)/shard_map/all_gather | solution.py:87
  1789.5 13.6 convolution_convert_fusion.4
  1803.2 14.9 fusion.68
  1818.0 15.1 fusion.65
  1852.6 14.8 reduce-scatter.23.cloned.1.call-done
  1872.1 159.5 %all-reduce.4.cloned.1.call-done = (bf16[576,288]{1,0:T(8,128)(2,1)}, bf16[576,288]{1,0:T(8,128)(2,1)}, bf16[576,288]{1,0:T(8,128)(2,1)}, bf16[288,576]{1,0:T(8,...) async-done(((bf16[576,288]{1,0:T(8,128)(2,1)}, bf16[576,288]{1,0:T(8,128)(2,1)}, bf16[576,288]{1,0:T(8,128)(2,1)}, bf16[288,576]{1,0:T(8,128)(2,1)}, ...) | async-done | bytes 3806224 | tf_op jit(solution)/shard_map/psum | solution.py:317
  2055.0 41.5 %all-reduce = (f32[1152]{0:T(1024)}, f32[1152]{0:T(1024)}, f32[1152]{0:T(1024)S(1)}, f32[1152]{0:T(1024)S(1)}, f32[1152]{0:T(1024)}, /*index=5*/f32[1152]{0:T(10...) all-reduce(f32[1152]{0:T(1024)S(1)} %get-tuple-element.309, ...), channel_id=1, replica_groups=mesh['dp'=4,'row'=2,'col'=4] {'dp','row','col'}, use_global_device_ids=true, to_apply=%region_23.24 | all-reduce | flops 13520 | bytes 108160 | tf_op jit(solution)/shard_map/psum | solution.py:296
  (300 shorter events, 423.9 us)
Async XLA Ops:
  7.2 577.9 %copy-start = (bf16[576,1076]{1,0:T(8,128)(2,1)S(1)}, bf16[576,1076]{1,0:T(8,128)(2,1)}, u32[]{:S(2)}) copy-start(bf16[576,1076]{1,0:T(8,128)(2,1)} %param.34) | copy-start | bytes 3718660
  7.2 117.1 %all-gather.21.cloned.1.call-start = ((), (), s32[]{:S(2)}) async-start(), calls=%async_computation.28 | async-start | bytes 8847360 | tf_op jit(solution)/shard_map/all_gather | solution.py:33
  72.7 188.6 %reduce-scatter.9.cloned.1.call-start = ((), (), s32[]{:S(2)}) async-start(), calls=%async_computation.16 | async-start | bytes 15826944 | tf_op jit(solution)/shard_map/reduce_scatter | solution.py:44
  73.5 65.0 %copy-start.11 = (bf16[576,288]{1,0:T(8,128)(2,1)}, bf16[576,288]{1,0:T(8,128)(2,1)S(1)}, u32[]{:S(2)}) copy-start(bf16[576,288]{1,0:T(8,128)(2,1)S(1)} %copy.178) | copy-start | bytes 995332
  73.8 64.8 %copy-start.13 = (bf16[576,288]{1,0:T(8,128)(2,1)}, bf16[576,288]{1,0:T(8,128)(2,1)S(1)}, u32[]{:S(2)}) copy-start(bf16[576,288]{1,0:T(8,128)(2,1)S(1)} %copy.179) | copy-start | bytes 995332
  74.0 64.5 %copy-start.15 = (bf16[576,288]{1,0:T(8,128)(2,1)}, bf16[576,288]{1,0:T(8,128)(2,1)S(1)}, u32[]{:S(2)}) copy-start(bf16[576,288]{1,0:T(8,128)(2,1)S(1)} %copy.180) | copy-start | bytes 995332
  138.6 227.3 %all-gather.13.cloned.1.call-start = ((), (), s32[]{:S(2)}) async-start(), calls=%async_computation.17 | async-start | bytes 5308416 | tf_op jit(solution)/shard_map/all_gather | solution.py:55
  283.5 82.4 %copy-start.39 = (bf16[288,576]{1,0:T(8,128)(2,1)S(1)}, bf16[288,576]{1,0:T(8,128)(2,1)}, u32[]{:S(2)}) copy-start(bf16[288,576]{1,0:T(8,128)(2,1)} %param.30) | copy-start | bytes 995332
  316.3 58.4 %copy-start.6 = (bf16[4,729,288]{1,2,0:T(8,128)(2,1)}, bf16[4,729,288]{1,2,0:T(8,128)(2,1)S(1)}, u32[]{:S(2)}) copy-start(bf16[4,729,288]{1,2,0:T(8,128)(2,1)S(1)} %get-tuple-element.600) | copy-start | bytes 5038852
  316.3 122.7 %reduce-scatter.11.cloned.1.call-start = ((), (), s32[]{:S(2)}) async-start(), calls=%async_computation.18 | async-start | bytes 8847360 | tf_op jit(solution)/shard_map/reduce_scatter | solution.py:60
  374.7 160.6 %all-gather.25.cloned.1.call-start = ((), (), s32[]{:S(2)}) async-start(), calls=%async_computation.30 | async-start | bytes 8847360 | tf_op jit(solution)/shard_map/all_gather | solution.py:33
  434.8 150.3 %all-gather.23.cloned.1.call-start = ((), (), s32[]{:S(2)}) async-start(), calls=%async_computation.29 | async-start | bytes 8847360 | tf_op jit(solution)/shard_map/all_gather | solution.py:33
  535.0 204.4 %reduce-scatter.17.cloned.1.call-start = ((), (), s32[]{:S(2)}) async-start(), calls=%async_computation.22 | async-start | bytes 19906560 | tf_op jit(solution)/shard_map/reduce_scatter | solution.py:68
  551.9 341.8 %reduce-scatter.13.cloned.1.call-start = ((), (), s32[]{:S(2)}) async-start(), calls=%async_computation.19 | async-start | bytes 19906560 | tf_op jit(solution)/shard_map/reduce_scatter | solution.py:44
  601.6 292.0 %copy-start.34 = (f32[1076]{0:T(1024)S(1)}, f32[1076]{0:T(1024)}, u32[]{:S(2)}) copy-start(f32[1076]{0:T(1024)} %param.35) | copy-start | bytes 12916
  601.7 469.4 %all-gather.17.cloned.1.call-start = ((), (), s32[]{:S(2)}) async-start(), calls=%async_computation.23 | async-start | bytes 19906560 | tf_op jit(solution)/shard_map/all_gather | solution.py:87
  910.8 321.7 %all-gather.15.cloned.1.call-start = ((), (), s32[]{:S(2)}) async-start(), calls=%async_computation.20 | async-start | bytes 19906560 | tf_op jit(solution)/shard_map/all_gather | solution.py:55
  911.4 387.9 %reduce-scatter.19.cloned.1.call-start = ((), (), s32[]{:S(2)}) async-start(), calls=%async_computation.24 | async-start | bytes 8847360 | tf_op jit(solution)/shard_map/reduce_scatter | solution.py:95
  1086.9 279.0 %reduce-scatter.15.cloned.1.call-start = ((), (), s32[]{:S(2)}) async-start(), calls=%async_computation.21 | async-start | bytes 8847360 | tf_op jit(solution)/shard_map/reduce_scatter | solution.py:60
  1299.3 66.6 %all-to-all-start.5 = ((bf16[2,729,576]{1,2,0:T(8,128)(2,1)}), bf16[2,729,576]{1,2,0:T(8,128)(2,1)S(1)}, u32[]{:S(2)}, u32[]{:S(2)}) async-start(bf16[2,729,576]{1,2,0:T(8,128)(2,1)} %reduce-scatter.19.cloned.1.call-done), calls=%async_computation.11 | async-start | bytes 3538944 | tf_op jit(solution)/shard_map/all_to_all | solution.py:37
  1365.9 26.2 %all-to-all-start.3 = ((bf16[2,729,576]{1,2,0:T(8,128)(2,1)}), bf16[2,729,576]{1,2,0:T(8,128)(2,1)}, u32[]{:S(2)}, u32[]{:S(2)}) async-start(bf16[2,729,576]{1,2,0:T(8,128)(2,1)} %reduce-scatter.15.cloned.1.call-done), calls=%async_computation.7 | async-start | bytes 3538944 | tf_op jit(solution)/shard_map/all_to_all | solution.py:37
  1370.6 147.3 %all-gather.27.cloned.1.call-start = ((), (), s32[]{:S(2)}) async-start(), calls=%async_computation.31 | async-start | bytes 8847360 | tf_op jit(solution)/shard_map/all_gather | solution.py:33
  1467.8 105.7 %reduce-scatter.21.cloned.1.call-start = ((), (), s32[]{:S(2)}) async-start(), calls=%async_computation.25 | async-start | bytes 5308416 | tf_op jit(solution)/shard_map/reduce_scatter | solution.py:68
  1525.6 263.9 %all-gather.19.cloned.1.call-start = ((), (), s32[]{:S(2)}) async-start(), calls=%async_computation.26 | async-start | bytes 15826944 | tf_op jit(solution)/shard_map/all_gather | solution.py:87
  1659.1 130.4 %copy-start.12 = (bf16[576,288]{1,0:T(8,128)(2,1)S(1)}, bf16[576,288]{1,0:T(8,128)(2,1)}, u32[]{:S(2)}) copy-start(bf16[576,288]{1,0:T(8,128)(2,1)} %copy-done.11) | copy-start | bytes 995332
  1659.1 130.4 %copy-start.14 = (bf16[576,288]{1,0:T(8,128)(2,1)S(1)}, bf16[576,288]{1,0:T(8,128)(2,1)}, u32[]{:S(2)}) copy-start(bf16[576,288]{1,0:T(8,128)(2,1)} %copy-done.13) | copy-start | bytes 995332
  1659.1 130.4 %copy-start.16 = (bf16[576,288]{1,0:T(8,128)(2,1)S(1)}, bf16[576,288]{1,0:T(8,128)(2,1)}, u32[]{:S(2)}) copy-start(bf16[576,288]{1,0:T(8,128)(2,1)} %copy-done.15) | copy-start | bytes 995332
  1659.1 208.3 %reduce-scatter.23.cloned.1.call-start = ((), (), s32[]{:S(2)}) async-start(), calls=%async_computation.27 | async-start | bytes 8847360 | tf_op jit(solution)/shard_map/reduce_scatter | solution.py:95
  1803.1 228.5 %all-reduce.4.cloned.1.call-start = ((), (), s32[]{:S(2)}) async-start(), calls=%async_computation.32 | async-start | bytes 8699904 | tf_op jit(solution)/shard_map/psum | solution.py:317
  1803.1 37.8 %slice-start = ((s8[10551296]{0:T(1024)(128)(4,1)}), s8[4194304]{0:T(1024)(128)(4,1)S(1)}, s32[]{:S(2)}) async-start(s8[10551296]{0:T(1024)(128)(4,1)} %bitcast.269), calls=%async_computation.33 | async-start | bytes 8388608
  1803.1 37.8 %slice-start.1 = ((s8[10551296]{0:T(1024)(128)(4,1)}), s8[4194304]{0:T(1024)(128)(4,1)S(1)}, s32[]{:S(2)}) async-start(s8[10551296]{0:T(1024)(128)(4,1)} %bitcast.269), calls=%async_computation.34 | async-start | bytes 8388608
  1867.4 176.1 %all-to-all-start.7 = ((bf16[2,729,576]{1,2,0:T(8,128)(2,1)}), bf16[2,729,576]{1,2,0:T(8,128)(2,1)S(1)}, u32[]{:S(2)}, u32[]{:S(2)}) async-start(bf16[2,729,576]{1,2,0:T(8,128)(2,1)} %reduce-scatter.23.cloned.1.call-done), calls=%async_computation.15 | async-start | bytes 3538944 | tf_op jit(solution)/shard_map/all_to_all | solution.py:37
  (31 other events, 196.1 us)
Sparse Core Ops, SparseCore 0:
  72.9 51.3 all-gather.20
  138.7 122.6 reduce-scatter.8
  316.5 49.3 all-gather.12
  374.8 64.1 reduce-scatter.10
  440.5 50.8 all-gather.24
  535.1 49.8 all-gather.22
  587.4 151.9 reduce-scatter.16
  741.7 151.9 reduce-scatter.12
  910.9 160.0 all-gather.16
  1072.4 160.0 all-gather.14
  1235.0 64.1 reduce-scatter.18
  1301.7 64.1 reduce-scatter.14
  1467.9 49.9 all-gather.26
  1525.7 47.7 reduce-scatter.20
  1659.2 130.1 all-gather.18
  1803.2 64.1 reduce-scatter.22
  1871.3 160.2 all-reduce.3
where the time goes:
time: 2120 us; the launch traced here: 2110 us
  waiting for transfers between devices  1380 us (65%)
  matrix products  208 us (10%)
  local copies, waits for them, and re-layouts  194 us (9%)
  blocking collectives  163 us (8%)
  other arithmetic  135 us (6%)
    all_gather x2, waiting for transfers between devices, back_in(): piece = lax.all_gather(grad_bf, 'row', axis=0, tiled=True)  290 us
    reduce_scatter x2, waiting for transfers between devices, project_in(): lax.psum_scatter(jnp.dot(gathered, weight, preferred_element_type=jnp.flo...  277 us
    all_gather x2, waiting for transfers between devices, project_out(): lax.all_gather(block_bf, 'row', axis=0, tiled=True)  195 us
    reduce_scatter x2, waiting for transfers between devices, back_out(): lax.psum_scatter(lax.dot_general(grads_all, weight, contract_last, prefer...  185 us
    psum x1, waiting for transfers between devices, shards(): lax.psum(blocks[0].astype(jnp.bfloat16), 'dp').astype(jnp.float32)  159 us
    all_gather x4, waiting for transfers between devices, spread(): return lax.all_gather(feature_part, 'col', axis=0, tiled=True)  133 us
    all_to_all x4, blocking collectives, spread(): lax.all_to_all(block, 'row', split_axis=2, concat_axis=0, tiled=True)  96.1 us
    unnamed x106, local copies, waits for them, and re-layouts  77.6 us
  transfers between devices with their start and end apart: 20, of which 17 were waited for; matrix products, arithmetic and copies ran while one was open for 11% of the time, Pallas kernels for 0%

commit v1 on v0

--- a/solution.py
+++ b/solution.py
@@ -314,7 +314,7 @@
     value_bias_grad = lax.dynamic_slice_in_dim(totals[7], col_index * query_part, query_part, 0)
     expand_bias_grad = lax.dynamic_slice_in_dim(totals[8], col_index * expand_part, expand_part, 0)
     weight_totals = (
-        lax.psum(blocks[0].astype(jnp.bfloat16), "dp").astype(jnp.float32),
+        jnp.sum(lax.all_gather(blocks[0].astype(jnp.bfloat16), "dp"), axis=0).astype(jnp.float32),
         lax.psum(blocks[1].astype(jnp.bfloat16), "dp").astype(jnp.float32),
         lax.psum(blocks[2].astype(jnp.bfloat16), "dp").astype(jnp.float32),
         lax.psum(blocks[3].astype(jnp.bfloat16), "dp").astype(jnp.float32),

time: 2120 us -> 2140 us (level)
    all_gather x0 -> x1, waiting for transfers between devices: none -> 32.7 us  [shards(): lax.all_gather(blocks[0].astype(jnp.bfloat16), 'dp')]
    unnamed x106 -> x102, local copies, waits for them, and re-layouts: 77.6 us -> 77.8 us
    unnamed x5 -> x4, other arithmetic: 47.3 us -> 47.3 us
  transfers between devices with their start and end apart: 20 -> 21, of which waited for: 17 -> 18; matrix products, arithmetic and copies ran while one was open for 11% -> 11% of each run, Pallas kernels for 0% -> 0%
where the time goes in v1:
time: 2140 us; the launch traced here: 2130 us
  waiting for transfers between devices  1400 us (65%)
  matrix products  209 us (10%)
  local copies, waits for them, and re-layouts  194 us (9%)
  blocking collectives  163 us (8%)
  other arithmetic  138 us (6%)
    all_gather x2, waiting for transfers between devices, back_in(): piece = lax.all_gather(grad_bf, 'row', axis=0, tiled=True)  290 us
    reduce_scatter x2, waiting for transfers between devices, project_in(): lax.psum_scatter(jnp.dot(gathered, weight, preferred_element_type=jnp.flo...  277 us
    all_gather x2, waiting for transfers between devices, project_out(): lax.all_gather(block_bf, 'row', axis=0, tiled=True)  195 us
    reduce_scatter x2, waiting for transfers between devices, back_out(): lax.psum_scatter(lax.dot_general(grads_all, weight, contract_last, prefer...  185 us
    psum x1, waiting for transfers between devices, shards(): lax.psum(blocks[1].astype(jnp.bfloat16), 'dp').astype(jnp.float32)  146 us
    all_gather x4, waiting for transfers between devices, spread(): return lax.all_gather(feature_part, 'col', axis=0, tiled=True)  133 us
    all_to_all x4, blocking collectives, spread(): lax.all_to_all(block, 'row', split_axis=2, concat_axis=0, tiled=True)  96.1 us
    unnamed x102, local copies, waits for them, and re-layouts  77.8 us
  transfers between devices with their start and end apart: 21, of which 18 were waited for; matrix products, arithmetic and copies ran while one was open for 11% of the time, Pallas kernels for 0%

profile of v1, /device:TPU:0, one launch (start us, length us, event | category | flops | bytes accessed | tf_op | source)
XLA Modules:
  0.0 2130.7 jit_solution(14610354786384665175)
XLA Ops:
  38.0 25.5 %all_to_all.118 = bf16[2,2,209952]{2,1,0:T(2,128)(2,1)S(1)} all-to-all(bf16[2,2,209952]{2,1,0:T(2,128)(2,1)} %reshape.491), channel_id=1, replica_groups=mesh['dp'=4,'row'=2,'col'=4] {'row'}, dimensions={0} | all-to-all | bytes 3359232 | tf_op jit(solution)/shard_map/all_to_all | solution.py:32
  73.9 50.4 %all-gather.24.cloned.1.call-done = bf16[8,1,729,576]{2,3,1,0:T(8,128)(2,1)} async-done(((bf16[2,1,729,576]{2,3,1,0:T(8,128)(2,1)}), bf16[8,1,729,576]{2,3,1,0:T(8,128)(2,1)}) %all-gather.24.cloned.1.call-update) | async-done | bytes 6718480 | tf_op jit(solution)/shard_map/all_gather | solution.py:33
  124.3 14.3 fusion.37
  139.2 122.2 %reduce-scatter.9.cloned.1.call-done = bf16[4,729,864]{2,1,0:T(8,128)(2,1)} async-done(((bf16[8,729,864]{2,1,0:T(8,128)(2,1)}), bf16[4,729,864]{2,1,0:T(8,128)(2,1)}) %reduce-scatter.9.cloned.1.call-update) | async-done | bytes 5038864 | tf_op jit(solution)/shard_map/reduce_scatter | solution.py:44
  283.6 32.8 %while.26 = (s32[]{:T(128)}, bf16[4,729,288]{1,2,0:T(8,128)(2,1)}, f32[4,4,729,1]{2,1,3,0:T(4,128)}, bf16[4,729,288]{1,2,0:T(8,128)(2,1)}, bf16[4,729,288]{1,2,0...) while((s32[]{:T(128)}, bf16[4,729,288]{1,2,0:T(8,128)(2,1)}, f32[4,4,729,1]{2,1,3,0:T(4,128)}, ...), condition=%wide.region_6.7_spmd, body=%wide.region_3.6_spmd.sunk | while | flops 629433152 | bytes 30664516 | solution.py:128
  316.6 49.3 %all-gather.16.cloned.1.call-done = bf16[8,729,288]{1,2,0:T(8,128)(2,1)} async-done(((bf16[4,729,288]{1,2,0:T(8,128)(2,1)}), bf16[8,729,288]{1,2,0:T(8,128)(2,1)}) %all-gather.16.cloned.1.call-update) | async-done | bytes 3359248 | tf_op jit(solution)/shard_map/all_gather | solution.py:55
  401.6 24.2 %all_to_all.119 = bf16[2,2,209952]{2,1,0:T(2,128)(2,1)S(1)} all-to-all(bf16[2,2,209952]{2,1,0:T(2,128)(2,1)} %reshape.493), channel_id=1, replica_groups=mesh['dp'=4,'row'=2,'col'=4] {'row'}, dimensions={0} | all-to-all | bytes 3359232 | tf_op jit(solution)/shard_map/all_to_all | solution.py:32
  439.1 25.3 %all_to_all.120 = bf16[2,729,576]{1,2,0:T(8,128)(2,1)S(1)} all-to-all(bf16[2,729,576]{1,2,0:T(8,128)(2,1)} %reduce-scatter.11.cloned.1.call-done), channel_id=1, replica_groups=mesh['dp'=4,'row'=2,'col'=4] {'row'}, dimensions={0} | all-to-all | bytes 3359232 | tf_op jit(solution)/shard_map/all_to_all | solution.py:37
  502.1 23.4 %all_to_all.121 = bf16[2,2,209952]{2,1,0:T(2,128)(2,1)S(1)} all-to-all(bf16[2,2,209952]{2,1,0:T(2,128)(2,1)} %reshape.495), channel_id=1, replica_groups=mesh['dp'=4,'row'=2,'col'=4] {'row'}, dimensions={0} | all-to-all | bytes 3359232 | tf_op jit(solution)/shard_map/all_to_all | solution.py:32
  535.4 16.7 convolution_convert_fusion
  552.1 32.8 %all-gather.26.cloned.1.call-done = bf16[8,1,729,576]{2,3,1,0:T(8,128)(2,1)} async-done(((bf16[2,1,729,576]{2,3,1,0:T(8,128)(2,1)}), bf16[8,1,729,576]{2,3,1,0:T(8,128)(2,1)}) %all-gather.26.cloned.1.call-update) | async-done | bytes 6718480 | tf_op jit(solution)/shard_map/all_gather | solution.py:33
  585.0 16.6 convolution_convert_fusion.1
  601.6 137.6 %reduce-scatter.17.cloned.1.call-done = bf16[4,729,1076]{1,2,0:T(8,128)(2,1)} async-done(((bf16[8,729,1076]{1,2,0:T(8,128)(2,1)}), bf16[4,729,1076]{1,2,0:T(8,128)(2,1)}) %reduce-scatter.17.cloned.1.call-update) | async-done | bytes 6275248 | tf_op jit(solution)/shard_map/reduce_scatter | solution.py:68
  739.3 154.3 %reduce-scatter.13.cloned.1.call-done = bf16[4,729,1076]{1,2,0:T(8,128)(2,1)} async-done(((bf16[8,729,1076]{1,2,0:T(8,128)(2,1)}), bf16[4,729,1076]{1,2,0:T(8,128)(2,1)}) %reduce-scatter.13.cloned.1.call-update) | async-done | bytes 6275248 | tf_op jit(solution)/shard_map/reduce_scatter | solution.py:44
  893.6 17.1 fusion.91
  911.5 159.4 %all-gather.20.cloned.1.call-done = bf16[8,729,1076]{1,2,0:T(8,128)(2,1)} async-done(((bf16[4,729,1076]{1,2,0:T(8,128)(2,1)}), bf16[8,729,1076]{1,2,0:T(8,128)(2,1)}) %all-gather.20.cloned.1.call-update) | async-done | bytes 12550480 | tf_op jit(solution)/shard_map/all_gather | solution.py:87
  1070.9 15.9 convolution_convert_fusion.2
  1086.9 145.5 %all-gather.18.cloned.1.call-done = bf16[8,729,1076]{1,2,0:T(8,128)(2,1)} async-done(((bf16[4,729,1076]{1,2,0:T(8,128)(2,1)}), bf16[8,729,1076]{1,2,0:T(8,128)(2,1)}) %all-gather.18.cloned.1.call-update) | async-done | bytes 12550480 | tf_op jit(solution)/shard_map/all_gather | solution.py:55
  1232.4 15.9 convolution_convert_fusion.3
  1248.3 50.8 %reduce-scatter.19.cloned.1.call-done = bf16[2,729,576]{1,2,0:T(8,128)(2,1)} async-done(((bf16[8,729,576]{1,2,0:T(8,128)(2,1)}), bf16[2,729,576]{1,2,0:T(8,128)(2,1)}) %reduce-scatter.19.cloned.1.call-update) | async-done | bytes 1679632 | tf_op jit(solution)/shard_map/reduce_scatter | solution.py:95
  1303.0 62.8 %reduce-scatter.15.cloned.1.call-done = bf16[2,729,576]{1,2,0:T(8,128)(2,1)} async-done(((bf16[8,729,576]{1,2,0:T(8,128)(2,1)}), bf16[2,729,576]{1,2,0:T(8,128)(2,1)}) %reduce-scatter.15.cloned.1.call-update) | async-done | bytes 1679632 | tf_op jit(solution)/shard_map/reduce_scatter | solution.py:60
  1437.5 23.0 %all_to_all.122 = bf16[2,2,209952]{2,1,0:T(2,128)(2,1)} all-to-all(bf16[2,2,209952]{2,1,0:T(2,128)(2,1)S(1)} %reshape.497), channel_id=1, replica_groups=mesh['dp'=4,'row'=2,'col'=4] {'row'}, dimensions={0} | all-to-all | bytes 3359232 | tf_op jit(solution)/shard_map/all_to_all | solution.py:32
  1468.1 49.6 %all-gather.30.cloned.1.call-done = bf16[8,1,729,576]{2,3,1,0:T(8,128)(2,1)} async-done(((bf16[2,1,729,576]{2,3,1,0:T(8,128)(2,1)}), bf16[8,1,729,576]{2,3,1,0:T(8,128)(2,1)}) %all-gather.30.cloned.1.call-update) | async-done | bytes 6718480 | tf_op jit(solution)/shard_map/all_gather | solution.py:33
  1525.5 47.8 %reduce-scatter.21.cloned.1.call-done = bf16[4,729,288]{1,2,0:T(8,128)(2,1)} async-done(((bf16[8,729,288]{1,2,0:T(8,128)(2,1)}), bf16[4,729,288]{1,2,0:T(8,128)(2,1)}) %reduce-scatter.21.cloned.1.call-update) | async-done | bytes 1679632 | tf_op jit(solution)/shard_map/reduce_scatter | solution.py:68
  1573.3 70.2 %while.27 = (s32[]{:T(128)}, f32[4,729,288]{1,2,0:T(8,128)}, bf16[4,729,288]{1,2,0:T(8,128)(2,1)}, f32[4,729,288]{1,2,0:T(8,128)S(1)}, bf16[4,729,288]{1,2,0:T(8...) while((s32[]{:T(128)}, f32[4,729,288]{1,2,0:T(8,128)}, ...), condition=%wide.region_18.19_spmd, body=%wide.region_17.18_spmd.sunk | while | flops 1549022848 | bytes 52812796 | solution.py:172
  1658.9 130.3 %all-gather.22.cloned.1.call-done = bf16[8,729,864]{2,1,0:T(8,128)(2,1)} async-done(((bf16[4,729,864]{2,1,0:T(8,128)(2,1)}), bf16[8,729,864]{2,1,0:T(8,128)(2,1)}) %all-gather.22.cloned.1.call-update) | async-done | bytes 10077712 | tf_op jit(solution)/shard_map/all_gather | solution.py:87
  1789.2 13.6 convolution_convert_fusion.4
  1803.1 14.7 fusion.65
  1833.5 14.8 fusion.68
  1871.9 32.7 %all-gather.32.cloned.1.call-done = bf16[4,576,288]{1,2,0:T(8,128)(2,1)} async-done(((bf16[1,576,288]{1,2,0:T(8,128)(2,1)}), bf16[4,576,288]{1,2,0:T(8,128)(2,1)}) %all-gather.32.cloned.1.call-update) | async-done | bytes 1327120 | tf_op jit(solution)/shard_map/all_gather | solution.py:317
  1907.6 145.7 %all-reduce.4.cloned.1.call-done = (bf16[576,288]{1,0:T(8,128)(2,1)}, bf16[576,288]{1,0:T(8,128)(2,1)}, bf16[288,576]{1,0:T(8,128)(2,1)}, bf16[576,1076]{1,0:T(8,128)(2,1)}, bf16[1076,576]{0,1:T(8,128)(2,1)}) async-done(((bf16[576,288]{1,0:T(8,128)(2,1)}, bf16[576,288]{1,0:T(8,128)(2,1)}, bf16[288,576]{1,0:T(8,128)(2,1)}, bf16[576,1076]{1,0:T(8,128)(2,1)}, bf16[1076,576]{0,1:T(8,128)(2,1)}), ...) | async-done | bytes 3474448 | tf_op jit(solution)/shard_map/psum | solution.py:318
  2075.6 41.5 %all-reduce = (f32[1152]{0:T(1024)}, f32[1152]{0:T(1024)}, f32[1152]{0:T(1024)S(1)}, f32[1152]{0:T(1024)S(1)}, f32[1152]{0:T(1024)}, /*index=5*/f32[1152]{0:T(10...) all-reduce(f32[1152]{0:T(1024)S(1)} %get-tuple-element.309, ...), channel_id=1, replica_groups=mesh['dp'=4,'row'=2,'col'=4] {'dp','row','col'}, use_global_device_ids=true, to_apply=%region_23.24 | all-reduce | flops 13520 | bytes 108160 | tf_op jit(solution)/shard_map/psum | solution.py:296
  (299 shorter events, 441.6 us)
Async XLA Ops:
  7.2 577.8 %copy-start = (bf16[576,1076]{1,0:T(8,128)(2,1)S(1)}, bf16[576,1076]{1,0:T(8,128)(2,1)}, u32[]{:S(2)}) copy-start(bf16[576,1076]{1,0:T(8,128)(2,1)} %param.34) | copy-start | bytes 3718660
  7.2 117.1 %all-gather.24.cloned.1.call-start = ((), (), s32[]{:S(2)}) async-start(), calls=%async_computation.28 | async-start | bytes 8847360 | tf_op jit(solution)/shard_map/all_gather | solution.py:33
  72.8 188.7 %reduce-scatter.9.cloned.1.call-start = ((), (), s32[]{:S(2)}) async-start(), calls=%async_computation.16 | async-start | bytes 15826944 | tf_op jit(solution)/shard_map/reduce_scatter | solution.py:44
  73.4 65.2 %copy-start.11 = (bf16[576,288]{1,0:T(8,128)(2,1)}, bf16[576,288]{1,0:T(8,128)(2,1)S(1)}, u32[]{:S(2)}) copy-start(bf16[576,288]{1,0:T(8,128)(2,1)S(1)} %copy.182) | copy-start | bytes 995332
  73.6 64.9 %copy-start.13 = (bf16[576,288]{1,0:T(8,128)(2,1)}, bf16[576,288]{1,0:T(8,128)(2,1)S(1)}, u32[]{:S(2)}) copy-start(bf16[576,288]{1,0:T(8,128)(2,1)S(1)} %copy.183) | copy-start | bytes 995332
  73.9 64.7 %copy-start.15 = (bf16[576,288]{1,0:T(8,128)(2,1)}, bf16[576,288]{1,0:T(8,128)(2,1)S(1)}, u32[]{:S(2)}) copy-start(bf16[576,288]{1,0:T(8,128)(2,1)S(1)} %copy.184) | copy-start | bytes 995332
  138.6 227.3 %all-gather.16.cloned.1.call-start = ((), (), s32[]{:S(2)}) async-start(), calls=%async_computation.17 | async-start | bytes 5308416 | tf_op jit(solution)/shard_map/all_gather | solution.py:55
  283.6 82.3 %copy-start.39 = (bf16[288,576]{1,0:T(8,128)(2,1)S(1)}, bf16[288,576]{1,0:T(8,128)(2,1)}, u32[]{:S(2)}) copy-start(bf16[288,576]{1,0:T(8,128)(2,1)} %param.30) | copy-start | bytes 995332
  316.4 58.3 %copy-start.6 = (bf16[4,729,288]{1,2,0:T(8,128)(2,1)}, bf16[4,729,288]{1,2,0:T(8,128)(2,1)S(1)}, u32[]{:S(2)}) copy-start(bf16[4,729,288]{1,2,0:T(8,128)(2,1)S(1)} %get-tuple-element.598) | copy-start | bytes 5038852
  316.4 122.7 %reduce-scatter.11.cloned.1.call-start = ((), (), s32[]{:S(2)}) async-start(), calls=%async_computation.18 | async-start | bytes 8847360 | tf_op jit(solution)/shard_map/reduce_scatter | solution.py:60
  374.7 160.6 %all-gather.28.cloned.1.call-start = ((), (), s32[]{:S(2)}) async-start(), calls=%async_computation.30 | async-start | bytes 8847360 | tf_op jit(solution)/shard_map/all_gather | solution.py:33
  434.9 150.0 %all-gather.26.cloned.1.call-start = ((), (), s32[]{:S(2)}) async-start(), calls=%async_computation.29 | async-start | bytes 8847360 | tf_op jit(solution)/shard_map/all_gather | solution.py:33
  534.9 204.4 %reduce-scatter.17.cloned.1.call-start = ((), (), s32[]{:S(2)}) async-start(), calls=%async_computation.22 | async-start | bytes 19906560 | tf_op jit(solution)/shard_map/reduce_scatter | solution.py:68
  552.1 341.5 %reduce-scatter.13.cloned.1.call-start = ((), (), s32[]{:S(2)}) async-start(), calls=%async_computation.19 | async-start | bytes 19906560 | tf_op jit(solution)/shard_map/reduce_scatter | solution.py:44
  601.5 292.0 %copy-start.33 = (f32[1076]{0:T(1024)S(1)}, f32[1076]{0:T(1024)}, u32[]{:S(2)}) copy-start(f32[1076]{0:T(1024)} %param.35) | copy-start | bytes 12916
  601.6 469.4 %all-gather.20.cloned.1.call-start = ((), (), s32[]{:S(2)}) async-start(), calls=%async_computation.23 | async-start | bytes 19906560 | tf_op jit(solution)/shard_map/all_gather | solution.py:87
  910.7 321.7 %all-gather.18.cloned.1.call-start = ((), (), s32[]{:S(2)}) async-start(), calls=%async_computation.20 | async-start | bytes 19906560 | tf_op jit(solution)/shard_map/all_gather | solution.py:55
  911.3 387.9 %reduce-scatter.19.cloned.1.call-start = ((), (), s32[]{:S(2)}) async-start(), calls=%async_computation.24 | async-start | bytes 8847360 | tf_op jit(solution)/shard_map/reduce_scatter | solution.py:95
  1086.9 278.9 %reduce-scatter.15.cloned.1.call-start = ((), (), s32[]{:S(2)}) async-start(), calls=%async_computation.21 | async-start | bytes 8847360 | tf_op jit(solution)/shard_map/reduce_scatter | solution.py:60
  1299.2 66.6 %all-to-all-start.5 = ((bf16[2,729,576]{1,2,0:T(8,128)(2,1)}), bf16[2,729,576]{1,2,0:T(8,128)(2,1)S(1)}, u32[]{:S(2)}, u32[]{:S(2)}) async-start(bf16[2,729,576]{1,2,0:T(8,128)(2,1)} %reduce-scatter.19.cloned.1.call-done), calls=%async_computation.11 | async-start | bytes 3538944 | tf_op jit(solution)/shard_map/all_to_all | solution.py:37
  1365.8 26.2 %all-to-all-start.3 = ((bf16[2,729,576]{1,2,0:T(8,128)(2,1)}), bf16[2,729,576]{1,2,0:T(8,128)(2,1)}, u32[]{:S(2)}, u32[]{:S(2)}) async-start(bf16[2,729,576]{1,2,0:T(8,128)(2,1)} %reduce-scatter.15.cloned.1.call-done), calls=%async_computation.7 | async-start | bytes 3538944 | tf_op jit(solution)/shard_map/all_to_all | solution.py:37
  1370.5 147.2 %all-gather.30.cloned.1.call-start = ((), (), s32[]{:S(2)}) async-start(), calls=%async_computation.31 | async-start | bytes 8847360 | tf_op jit(solution)/shard_map/all_gather | solution.py:33
  1467.6 105.7 %reduce-scatter.21.cloned.1.call-start = ((), (), s32[]{:S(2)}) async-start(), calls=%async_computation.25 | async-start | bytes 5308416 | tf_op jit(solution)/shard_map/reduce_scatter | solution.py:68
  1525.4 263.8 %all-gather.22.cloned.1.call-start = ((), (), s32[]{:S(2)}) async-start(), calls=%async_computation.26 | async-start | bytes 15826944 | tf_op jit(solution)/shard_map/all_gather | solution.py:87
  1658.8 130.4 %copy-start.12 = (bf16[576,288]{1,0:T(8,128)(2,1)S(1)}, bf16[576,288]{1,0:T(8,128)(2,1)}, u32[]{:S(2)}) copy-start(bf16[576,288]{1,0:T(8,128)(2,1)} %copy-done.11) | copy-start | bytes 995332
  1658.8 130.4 %copy-start.14 = (bf16[576,288]{1,0:T(8,128)(2,1)S(1)}, bf16[576,288]{1,0:T(8,128)(2,1)}, u32[]{:S(2)}) copy-start(bf16[576,288]{1,0:T(8,128)(2,1)} %copy-done.13) | copy-start | bytes 995332
  1658.8 130.4 %copy-start.16 = (bf16[576,288]{1,0:T(8,128)(2,1)S(1)}, bf16[576,288]{1,0:T(8,128)(2,1)}, u32[]{:S(2)}) copy-start(bf16[576,288]{1,0:T(8,128)(2,1)} %copy-done.15) | copy-start | bytes 995332
  1658.8 208.4 %reduce-scatter.23.cloned.1.call-start = ((), (), s32[]{:S(2)}) async-start(), calls=%async_computation.27 | async-start | bytes 8847360 | tf_op jit(solution)/shard_map/reduce_scatter | solution.py:95
  1802.8 101.7 %all-gather.32.cloned.1.call-start = ((), (), s32[]{:S(2)}) async-start(), calls=%async_computation.32 | async-start | bytes 1843200 | tf_op jit(solution)/shard_map/all_gather | solution.py:317
  1833.2 220.1 %all-reduce.4.cloned.1.call-start = ((), (), s32[]{:S(2)}) async-start(), calls=%async_computation.33 | async-start | bytes 7815168 | tf_op jit(solution)/shard_map/psum | solution.py:318
  1854.3 17.1 copy-start.30
  1867.2 197.0 %all-to-all-start.7 = ((bf16[2,729,576]{1,2,0:T(8,128)(2,1)}), bf16[2,729,576]{1,2,0:T(8,128)(2,1)S(1)}, u32[]{:S(2)}, u32[]{:S(2)}) async-start(bf16[2,729,576]{1,2,0:T(8,128)(2,1)} %reduce-scatter.23.cloned.1.call-done), calls=%async_computation.15 | async-start | bytes 3538944 | tf_op jit(solution)/shard_map/all_to_all | solution.py:37
  (29 other events, 159.3 us)
Sparse Core Ops, SparseCore 0:
  72.9 51.3 all-gather.23
  138.7 122.6 reduce-scatter.8
  316.5 49.3 all-gather.15
  374.8 64.1 reduce-scatter.10
  440.5 50.8 all-gather.27
  535.0 49.8 all-gather.25
  587.3 151.9 reduce-scatter.16
  741.6 151.9 reduce-scatter.12
  910.8 160.0 all-gather.19
  1072.3 160.0 all-gather.17
  1235.0 64.1 reduce-scatter.18
  1301.6 64.1 reduce-scatter.14
  1467.7 49.8 all-gather.29
  1525.5 47.7 reduce-scatter.20
  1659.0 130.1 all-gather.21
  1803.0 64.1 reduce-scatter.22
  1869.2 35.3 all-gather.31
  1908.3 145.0 all-reduce.3
